TPU v7x, 128 devices: a whole 4x4x4 slice. The times are simulated.
128 devices in a mesh: band: 8 (over x, core), grid: 16 (over z, y).
Axes of the slice: x: 4, y: 4, z: 4, core: 2. Of those that a mesh axis runs over, the one named last changes fastest.
Arguments:
- orbitals: bfloat16 [32768, 2048], P('grid', 'band'), may hold values from -6 to 6
- projectors: bfloat16 [128, 8, 128], replicated, may hold values from -0.5 to 0.5
- sphere_start: int32 [128], replicated, may hold values from 0 to 1920, as said below
- proj_count: int32 [128], replicated, may hold values from 1 to 8
- owner_slab: int32 [128], replicated, may hold values from 0 to 15, as said below
- correlation_coef: float32 [128, 8, 8], replicated, as said below
Outputs:
- rotated: bfloat16 [32768, 2048], P(('grid', 'band'))
Inputs may be any that keep to these rules, and one draw needn't show every extreme that they name: `sphere_start`: a multiple of 128. `owner_slab`: every slab owns exactly 8 atoms. `correlation_coef`: each atom's matrix is symmetric positive definite.
All inputs are finite; a program needn't handle non-finite values.
Results may differ from a plain program's by a relative error of at most 0.0049.
Values may be sent and summed in bfloat16 or wider, within the bound.
A program may use at most 128 MiB of HBM per device.

v0:
```python
import jax
import jax.numpy as jnp
from jax import lax
from jax.sharding import PartitionSpec as P

SPH = 128
NPMAX = 8
A_SLAB = 8


def inverse_factor(matrix):
    order = matrix.shape[0]
    if order <= 512 or order % 2 != 0:
        lower = jnp.linalg.cholesky(matrix)
        identity = jnp.eye(order, dtype=matrix.dtype)
        return lax.linalg.triangular_solve(lower, identity, left_side=True, lower=True)
    half = order // 2
    upper_inv = inverse_factor(matrix[:half, :half])
    below = jnp.dot(matrix[half:, :half], upper_inv.T, precision=lax.Precision.HIGHEST)
    schur = matrix[half:, half:] - jnp.dot(below, below.T, precision=lax.Precision.HIGHEST)
    lower_inv = inverse_factor(schur)
    corner = -jnp.dot(
        lower_inv,
        jnp.dot(below, upper_inv, precision=lax.Precision.HIGHEST),
        precision=lax.Precision.HIGHEST,
    )
    top = jnp.concatenate([upper_inv, jnp.zeros((half, order - half), matrix.dtype)], axis=1)
    bottom = jnp.concatenate([corner, lower_inv], axis=1)
    return jnp.concatenate([top, bottom], axis=0)


def slab_atoms(owner_slab, slab):
    atoms = owner_slab.shape[0]
    keyed = jnp.where(owner_slab == slab, 0, 1) * atoms + jnp.arange(atoms, dtype=jnp.int32)
    return jnp.argsort(keyed, stable=True)[:A_SLAB]


def atom_terms(source, weights, starts, counts, coefs, valid):

    def take_rows(offset):
        return lax.dynamic_slice_in_dim(source, offset, SPH, 0)

    sphere_rows = jax.vmap(take_rows)(starts)
    correlations = jnp.einsum(
        "aij,ajn->ain", weights, sphere_rows, preferred_element_type=jnp.float32
    )
    active = (jnp.arange(NPMAX)[None, :] < counts[:, None]) & valid[:, None]
    correlations = jnp.where(active[:, :, None], correlations, jnp.zeros_like(correlations))
    weighted = jnp.einsum("aij,ajn->ain", coefs, correlations, precision=lax.Precision.HIGHEST)
    return (correlations, weighted)


def shards(orbitals, projectors, sphere_start, proj_count, owner_slab, correlation_coef):
    band_index = lax.axis_index("band")
    slab = lax.axis_index("grid")
    nbands = lax.axis_size("band")
    total_rows = orbitals.shape[0] * lax.axis_size("grid")
    chosen = slab_atoms(owner_slab, slab)
    weights = projectors[chosen]
    counts = proj_count[chosen]
    coefs = correlation_coef[chosen]
    gathered = lax.all_gather(orbitals, "band", axis=1, tiled=True)
    width = orbitals.shape[1]
    width_all = gathered.shape[1]
    gram_panel = jnp.dot(orbitals.T, gathered, preferred_element_type=jnp.float32) * (
        1.0 / total_rows
    )
    valid = jnp.ones((A_SLAB,), dtype=bool)
    correlations, weighted = atom_terms(
        gathered, weights, sphere_start[chosen], counts, coefs, valid
    )
    panel_weighted = lax.dynamic_slice_in_dim(weighted, band_index * width, width, 2)
    paw = jnp.dot(
        panel_weighted.reshape(-1, width).T,
        correlations.reshape(-1, width_all),
        precision=lax.Precision.HIGHEST,
    )
    panel_total = lax.psum(gram_panel + paw, "grid")
    metric = lax.all_gather(panel_total, "band", axis=0, tiled=True)
    height = orbitals.shape[0] // nbands
    mine = lax.dynamic_slice_in_dim(gathered, band_index * height, height, 0)
    inverse = inverse_factor(metric).astype(jnp.bfloat16)
    return jnp.dot(mine, inverse.T, preferred_element_type=jnp.float32).astype(jnp.bfloat16)


def solution(mesh):
    in_specs = (P("grid", "band"), P(), P(), P(), P(), P())
    out_specs = P(("grid", "band"), None)
    return jax.shard_map(shards, mesh=mesh, in_specs=in_specs, out_specs=out_specs, check_vma=False)
```

profile of v0, /device:TPU:1, one launch (start us, length us, event | category | flops | bytes accessed | tf_op | source)
XLA Modules:
  0.0 1023.9 jit_solution(12298596556159580187)
XLA Ops:
  15.4 50.7 %all-gather.3.cloned.1.call-done = bf16[2048,2048]{1,0:T(8,128)(2,1)} async-done(((bf16[2048,256]{1,0:T(8,128)(2,1)}), bf16[2048,2048]{1,0:T(8,128)(2,1)}) %all-gather.3.cloned.1.call-update) | async-done | bytes 8388624 | tf_op jit(solution)/shard_map/all_gather | solution.py:62
  66.1 25.7 %while.9 = (s32[]{:T(128)}, bf16[2048,2048]{1,0:T(8,128)(2,1)}, s32[8,2]{0,1:T(2,128)S(1)}, bf16[8,128,2048]{2,1,0:T(8,128)(2,1)}, s32[]{:T(128)}) while((s32[]{:T(128)}, bf16[2048,2048]{1,0:T(8,128)(2,1)}, s32[8,2]{0,1:T(2,128)S(1)}, bf16[8,128,2048]{2,1,0:T(8,128)(2,1)}, s32[]{:T(128)}) %tuple.104), condition=%wide.while_cond.1, body=%wide.while_body.1.sunk | while | flops 2 | bytes 1049189 | solution.py:41
  105.5 90.3 %all-reduce.7.cloned.1.call-done = f32[256,2048]{0,1:T(8,128)} async-done(((f32[256,2048]{0,1:T(8,128)}), f32[256,2048]{0,1:T(8,128)}) %all-reduce.7.cloned.1.call-update) | async-done | bytes 2097168 | tf_op jit(solution)/shard_map/psum | solution.py:78
  196.0 87.6 %all-gather.5.cloned.1.call-done = f32[2048,2048]{0,1:T(8,128)} async-done(((f32[256,2048]{0,1:T(8,128)}), f32[2048,2048]{0,1:T(8,128)}) %all-gather.5.cloned.1.call-update) | async-done | bytes 16777232 | tf_op jit(solution)/shard_map/all_gather | solution.py:79
  286.7 11.7 %cholesky.462 = f32[128,128]{1,0:T(8,128)S(1)} custom-call(f32[128,128]{1,0:T(8,128)S(1)} %cholesky.746), custom_call_target="Cholesky" | custom-call | tf_op jit(solution)/shard_map/jit(cholesky)/cholesky | solution.py:14
  309.1 11.7 %cholesky.481 = f32[128,128]{1,0:T(8,128)S(1)} custom-call(f32[128,128]{1,0:T(8,128)S(1)} %cholesky.750), custom_call_target="Cholesky" | custom-call | tf_op jit(solution)/shard_map/jit(cholesky)/cholesky | solution.py:14
  331.8 11.7 %cholesky.502 = f32[128,128]{1,0:T(8,128)S(1)} custom-call(f32[128,128]{1,0:T(8,128)S(1)} %cholesky.755), custom_call_target="Cholesky" | custom-call | tf_op jit(solution)/shard_map/jit(cholesky)/cholesky | solution.py:14
  353.9 11.7 %cholesky.519 = f32[128,128]{1,0:T(8,128)S(1)} custom-call(f32[128,128]{1,0:T(8,128)S(1)} %convolution_subtract_fusion.25), custom_call_target="Cholesky" | custom-call | tf_op jit(solution)/shard_map/jit(cholesky)/cholesky | solution.py:14
  378.1 39.3 %custom-call.38 = f32[4,128,128]{1,2,0:T(8,128)S(1)} custom-call(f32[4,128,128]{2,1,0:T(8,128)S(1)} %get-tuple-element.43), custom_call_target="InvertDiagBlocksLowerTriangular" | custom-call | tf_op jit(solution)/shard_map/triangular_solve/custom-call.3 | solution.py:16
  435.1 12.1 %cholesky.534 = f32[128,128]{1,0:T(8,128)S(1)} custom-call(f32[128,128]{1,0:T(8,128)S(1)} %cholesky.759), custom_call_target="Cholesky" | custom-call | tf_op jit(solution)/shard_map/jit(cholesky)/cholesky | solution.py:14
  459.7 11.7 %cholesky.553 = f32[128,128]{1,0:T(8,128)S(1)} custom-call(f32[128,128]{1,0:T(8,128)S(1)} %cholesky.763), custom_call_target="Cholesky" | custom-call | tf_op jit(solution)/shard_map/jit(cholesky)/cholesky | solution.py:14
  482.8 11.9 %cholesky.574 = f32[128,128]{1,0:T(8,128)S(1)} custom-call(f32[128,128]{1,0:T(8,128)S(1)} %cholesky.768), custom_call_target="Cholesky" | custom-call | tf_op jit(solution)/shard_map/jit(cholesky)/cholesky | solution.py:14
  506.0 11.7 %cholesky.591 = f32[128,128]{1,0:T(8,128)S(1)} custom-call(f32[128,128]{1,0:T(8,128)S(1)} %convolution_subtract_fusion.24), custom_call_target="Cholesky" | custom-call | tf_op jit(solution)/shard_map/jit(cholesky)/cholesky | solution.py:14
  523.9 11.2 %while.11 = (s32[]{:T(128)}, f32[512,512]{1,0:T(8,128)}, s32[4,2]{0,1:T(2,128)S(1)}, f32[4,128,128]{2,1,0:T(8,128)S(1)}, s32[]{:T(128)}) while((s32[]{:T(128)}, f32[512,512]{1,0:T(8,128)}, s32[4,2]{0,1:T(2,128)S(1)}, f32[4,128,128]{2,1,0:T(8,128)S(1)}, s32[]{:T(128)}) %tuple.125), condition=%wide.while_cond.clone, body=%wide.while_body.clone.sunk | while | flops 2 | bytes 131189 | solution.py:16
  535.1 39.5 %custom-call.42 = f32[4,128,128]{1,2,0:T(8,128)S(1)} custom-call(f32[4,128,128]{2,1,0:T(8,128)S(1)} %get-tuple-element.44), custom_call_target="InvertDiagBlocksLowerTriangular" | custom-call | tf_op jit(solution)/shard_map/triangular_solve/custom-call.3 | solution.py:16
  590.3 28.5 %fusion.9 = f32[1024,1024]{1,0:T(8,128)S(1)} fusion(f32[2048,2048]{0,1:T(8,128)} %all-gather.5.cloned.1.call-done, f32[512,512]{1,0:T(8,128)S(1)} %copy-done.5, f32[128,512]{1,0:T(8,128)S(1)} %fusion.125, f32[128,512]{1,0:T(8,128)S(1)} %fusion.126, f32[128,512]{1,0:T(8,128)S(1)} %fusion.128, f32[128,512]{1,0:T(8,128)S(1)} %fusion.81, ...), kind=kOutput, calls=%fused_computation.24 | convolution fusion | flops 12892241920 | bytes 11534336 | tf_op jit(solution)/shard_map/dot_general | solution.py:19
  618.8 18.2 %slice_subtract_fusion = f32[1024,1024]{0,1:T(8,128)} fusion(f32[2048,2048]{0,1:T(8,128)} %all-gather.5.cloned.1.call-done, f32[1024,1024]{1,0:T(8,128)S(1)} %fusion.9), kind=kOutput, calls=%fused_computation.26 | convolution fusion | flops 12885950464 | bytes 16777216 | tf_op jit(solution)/shard_map/dot_general | solution.py:20
  643.3 11.7 %cholesky.606 = f32[128,128]{1,0:T(8,128)S(1)} custom-call(f32[128,128]{1,0:T(8,128)S(1)} %cholesky.772), custom_call_target="Cholesky" | custom-call | tf_op jit(solution)/shard_map/jit(cholesky)/cholesky | solution.py:14
  667.5 11.7 %cholesky.625 = f32[128,128]{1,0:T(8,128)S(1)} custom-call(f32[128,128]{1,0:T(8,128)S(1)} %cholesky.776), custom_call_target="Cholesky" | custom-call | tf_op jit(solution)/shard_map/jit(cholesky)/cholesky | solution.py:14
  691.1 11.7 %cholesky.646 = f32[128,128]{1,0:T(8,128)S(1)} custom-call(f32[128,128]{1,0:T(8,128)S(1)} %cholesky.781), custom_call_target="Cholesky" | custom-call | tf_op jit(solution)/shard_map/jit(cholesky)/cholesky | solution.py:14
  714.1 11.7 %cholesky.663 = f32[128,128]{1,0:T(8,128)S(1)} custom-call(f32[128,128]{1,0:T(8,128)S(1)} %convolution_subtract_fusion.23), custom_call_target="Cholesky" | custom-call | tf_op jit(solution)/shard_map/jit(cholesky)/cholesky | solution.py:14
  732.4 11.7 %while.12 = (s32[]{:T(128)}, f32[512,512]{1,0:T(8,128)}, s32[4,2]{0,1:T(2,128)S(1)}, f32[4,128,128]{2,1,0:T(8,128)S(1)}, s32[]{:T(128)}) while((s32[]{:T(128)}, f32[512,512]{1,0:T(8,128)}, s32[4,2]{0,1:T(2,128)S(1)}, f32[4,128,128]{2,1,0:T(8,128)S(1)}, s32[]{:T(128)}) %tuple.126), condition=%wide.while_cond.clone.1, body=%wide.while_body.clone.1.sunk | while | flops 2 | bytes 131189 | solution.py:16
  744.1 39.3 %custom-call.46 = f32[4,128,128]{1,2,0:T(8,128)S(1)} custom-call(f32[4,128,128]{2,1,0:T(8,128)S(1)} %get-tuple-element.45), custom_call_target="InvertDiagBlocksLowerTriangular" | custom-call | tf_op jit(solution)/shard_map/triangular_solve/custom-call.3 | solution.py:16
  801.2 17.2 %fusion.172 = f32[1024,1024]{1,0:T(8,128)} fusion(f32[1024,1024]{1,0:T(8,128)S(1)} %copy-done.17, f32[512,512]{1,0:T(8,128)S(1)} %copy-done.6, f32[128,512]{1,0:T(8,128)S(1)} %copy-done.12, f32[128,512]{1,0:T(8,128)S(1)} %fusion.126, f32[128,512]{1,0:T(8,128)S(1)} %fusion.128, f32[128,512]{1,0:T(8,128)S(1)} %fusion.81, f32[512,512]{1,0:T(8,128)S(1)} %copy-done.3), kind=kOutput, calls=%fused_computation.324 | convolution fusion | flops 12892241920 | bytes 11534336 | tf_op jit(solution)/shard_map/dot_general | solution.py:24
  822.1 11.7 %cholesky.678 = f32[128,128]{1,0:T(8,128)S(1)} custom-call(f32[128,128]{1,0:T(8,128)S(1)} %cholesky.785), custom_call_target="Cholesky" | custom-call | tf_op jit(solution)/shard_map/jit(cholesky)/cholesky | solution.py:14
  846.4 11.7 %cholesky.697 = f32[128,128]{1,0:T(8,128)S(1)} custom-call(f32[128,128]{1,0:T(8,128)S(1)} %cholesky.789), custom_call_target="Cholesky" | custom-call | tf_op jit(solution)/shard_map/jit(cholesky)/cholesky | solution.py:14
  869.6 11.7 %cholesky.718 = f32[128,128]{1,0:T(8,128)S(1)} custom-call(f32[128,128]{1,0:T(8,128)S(1)} %cholesky.794), custom_call_target="Cholesky" | custom-call | tf_op jit(solution)/shard_map/jit(cholesky)/cholesky | solution.py:14
  892.6 11.7 %cholesky.735 = f32[128,128]{1,0:T(8,128)S(1)} custom-call(f32[128,128]{1,0:T(8,128)S(1)} %convolution_subtract_fusion.22), custom_call_target="Cholesky" | custom-call | tf_op jit(solution)/shard_map/jit(cholesky)/cholesky | solution.py:14
  911.2 12.0 %while.13 = (s32[]{:T(128)}, f32[512,512]{1,0:T(8,128)}, s32[4,2]{0,1:T(2,128)S(1)}, f32[4,128,128]{2,1,0:T(8,128)S(1)}, s32[]{:T(128)}) while((s32[]{:T(128)}, f32[512,512]{1,0:T(8,128)}, s32[4,2]{0,1:T(2,128)S(1)}, f32[4,128,128]{2,1,0:T(8,128)S(1)}, s32[]{:T(128)}) %tuple.127), condition=%wide.while_cond.clone.2, body=%wide.while_body.clone.2.sunk | while | flops 2 | bytes 131189 | solution.py:16
  923.2 39.3 %custom-call.50 = f32[4,128,128]{1,2,0:T(8,128)S(1)} custom-call(f32[4,128,128]{2,1,0:T(8,128)S(1)} %get-tuple-element.46), custom_call_target="InvertDiagBlocksLowerTriangular" | custom-call | tf_op jit(solution)/shard_map/triangular_solve/custom-call.3 | solution.py:16
  976.3 13.6 %negate_convert_fusion = bf16[1024,1024]{1,0:T(8,128)(2,1)S(1)} fusion(f32[1024,1024]{1,0:T(8,128)S(1)} %copy-done.18, f32[512,512]{1,0:T(8,128)S(1)} %copy-done.7, f32[128,512]{1,0:T(8,128)S(1)} %fusion.113, f32[128,512]{1,0:T(8,128)S(1)} %fusion.114, f32[128,512]{1,0:T(8,128)S(1)} %fusion.116, f32[128,512]{1,0:T(8,128)S(1)} %fusion.77, ...), kind=kOutput, calls=%fused_computation.30 | convolution fusion | flops 12894339072 | bytes 9437184 | tf_op jit(solution)/shard_map/dot_general | solution.py:22
  990.0 26.9 %fusion.13 = bf16[256,2048]{1,0:T(8,128)(2,1)} fusion(bf16[1024,1024]{1,0:T(8,128)(2,1)S(1)} %copy-done.13, bf16[1024,1024]{1,0:T(8,128)(2,1)S(1)} %fusion.16, bf16[1024,1024]{1,0:T(8,128)(2,1)S(1)} %negate_convert_fusion, bf16[2048,2048]{1,0:T(8,128)(2,1)} %get-tuple-element.377, s32[]{:T(128)S(6)} %select_n.31), kind=kOutput, calls=%fused_computation.34 | convolution fusion | flops 2181562368 | bytes 8388612 | tf_op jit(solution)/shard_map/dot_general | solution.py:83
  (279 shorter events, 327.6 us)
Async XLA Ops:
  6.5 4.0 copy-start
  6.5 59.5 %all-gather.3.cloned.1.call-start = ((), (), s32[]{:S(2)}) async-start(), calls=%async_computation | async-start | bytes 9437184 | tf_op jit(solution)/shard_map/all_gather | solution.py:62
  7.3 188.6 %all-reduce.7.cloned.1.call-start = ((), (), s32[]{:S(2)}) async-start(), calls=%async_computation.1 | async-start | bytes 4194304 | tf_op jit(solution)/shard_map/psum | solution.py:78
  91.7 3.5 copy-start.14
  105.3 178.4 %all-gather.5.cloned.1.call-start = ((), (), s32[]{:S(2)}) async-start(), calls=%async_computation.2 | async-start | bytes 18874368 | tf_op jit(solution)/shard_map/all_gather | solution.py:79
  434.1 1.0 copy-start.8
  574.7 3.5 copy-start.15
  575.1 8.2 copy-start.5
  581.4 8.8 copy-start.11
  583.3 35.5 %copy-start.2 = (f32[512,512]{1,0:T(8,128)}, f32[512,512]{1,0:T(8,128)S(1)}, u32[]{:S(2)}) copy-start(f32[512,512]{1,0:T(8,128)S(1)} %convolution_negate_fusion.1) | copy-start | bytes 3145732
  618.8 18.2 %copy-start.16 = (f32[1024,1024]{1,0:T(8,128)}, f32[1024,1024]{1,0:T(8,128)S(1)}, u32[]{:S(2)}) copy-start(f32[1024,1024]{1,0:T(8,128)S(1)} %fusion.9) | copy-start | bytes 12582916
  642.3 1.0 copy-start.10
  793.9 7.3 copy-start.3
  794.0 7.3 copy-start.6
  794.0 7.2 copy-start.12
  794.0 7.2 copy-start.17
  821.1 1.0 copy-start.9
  909.8 58.6 %copy-start.4 = (f32[512,512]{1,0:T(8,128)S(1)}, f32[512,512]{1,0:T(8,128)}, u32[]{:S(2)}) copy-start(f32[512,512]{1,0:T(8,128)} %fusion.170) | copy-start | bytes 3145732
  962.9 7.4 copy-start.7
  968.5 7.9 copy-start.18
  976.3 13.7 %copy-start.13 = (bf16[1024,1024]{1,0:T(8,128)(2,1)S(1)}, bf16[1024,1024]{1,0:T(8,128)(2,1)}, u32[]{:S(2)}) copy-start(bf16[1024,1024]{1,0:T(8,128)(2,1)} %fusion.173) | copy-start | bytes 6291460
  990.0 26.9 %copy-start.1 = (bf16[128,8,128]{2,1,0:T(8,128)(2,1)S(1)}, bf16[128,8,128]{2,1,0:T(8,128)(2,1)}, u32[]{:S(2)}) copy-start(bf16[128,8,128]{2,1,0:T(8,128)(2,1)} %param.10) | copy-start | bytes 786436
Sparse Core Ops, SparseCore 0:
  9.0 57.0 all-gather.2
  105.4 90.4 all-reduce.6
  197.6 86.0 all-gather.4
where the time goes:
time: 1030 us; the launch traced here: 1020 us
  other arithmetic  503 us (49%)
  waiting for transfers between devices  229 us (22%)
  matrix products  182 us (18%)
  local copies, waits for them, and re-layouts  84.3 us (8%)
  between operations  25.2 us (2%)
    another operation x59, other arithmetic, inverse_factor(): lower = jnp.linalg.cholesky(matrix)  317 us
    another operation x11, other arithmetic, inverse_factor(): lax.linalg.triangular_solve(lower, identity, left_side=True, lower=True)  163 us
    psum x1, waiting for transfers between devices, shards(): panel_total = lax.psum(gram_panel + paw, 'grid')  90.3 us
    all_gather x1, waiting for transfers between devices, shards(): metric = lax.all_gather(panel_total, 'band', axis=0, tiled=True)  87.6 us
    all_gather x1, waiting for transfers between devices, shards(): gathered = lax.all_gather(orbitals, 'band', axis=1, tiled=True)  50.7 us
    another operation x53, local copies, waits for them, and re-layouts, inverse_factor(): lax.linalg.triangular_solve(lower, identity, left_side=True, lower=True)  42.3 us
    dot_general x3, matrix products, inverse_factor(): jnp.dot(matrix[half:, :half], upper_inv.T, precision=lax.Precision.HIGHEST)  38 us
    dot_general x1, matrix products, shards(): jnp.dot(mine, inverse.T, preferred_element_type=jnp.float32)  26.9 us
  transfers between devices with their start and end apart: 3, of which 3 were waited for; matrix products, arithmetic and copies ran while one was open for 1% of the time, Pallas kernels for 0%

commit v1 on v0

--- a/solution.py
+++ b/solution.py
@@ -75,7 +75,7 @@
         correlations.reshape(-1, width_all),
         precision=lax.Precision.HIGHEST,
     )
-    panel_total = lax.psum(gram_panel + paw, "grid")
+    panel_total = jnp.sum(lax.all_gather(gram_panel + paw, "grid"), axis=0)
     metric = lax.all_gather(panel_total, "band", axis=0, tiled=True)
     height = orbitals.shape[0] // nbands
     mine = lax.dynamic_slice_in_dim(gathered, band_index * height, height, 0)

time: 1030 us -> 1140 us (1.11)
  waiting for transfers between devices: 229 us -> 334 us
  other arithmetic: 503 us -> 515 us
    all_gather x0 -> x1, waiting for transfers between devices: none -> 198 us  [shards(): panel_total = jnp.sum(lax.all_gather(gram_panel + paw, 'grid'), axis=0)]
    psum x1 -> x0, waiting for transfers between devices: 90.3 us -> none  [shards(): panel_total = lax.psum(gram_panel + paw, 'grid')]
    reduce_sum x0 -> x1, other arithmetic: none -> 11.8 us  [shards(): panel_total = jnp.sum(lax.all_gather(gram_panel + paw, 'grid'), axis=0)]
where the time goes in v1:
time: 1140 us; the launch traced here: 1130 us
  other arithmetic  515 us (45%)
  waiting for transfers between devices  334 us (29%)
  matrix products  173 us (15%)
  local copies, waits for them, and re-layouts  87.8 us (8%)
  between operations  25.2 us (2%)
    another operation x59, other arithmetic, inverse_factor(): lower = jnp.linalg.cholesky(matrix)  317 us
    all_gather x1, waiting for transfers between devices, shards(): panel_total = jnp.sum(lax.all_gather(gram_panel + paw, 'grid'), axis=0)  198 us
    another operation x11, other arithmetic, inverse_factor(): lax.linalg.triangular_solve(lower, identity, left_side=True, lower=True)  163 us
    all_gather x1, waiting for transfers between devices, shards(): metric = lax.all_gather(panel_total, 'band', axis=0, tiled=True)  85 us
    all_gather x1, waiting for transfers between devices, shards(): gathered = lax.all_gather(orbitals, 'band', axis=1, tiled=True)  50.7 us
    another operation x53, local copies, waits for them, and re-layouts, inverse_factor(): lax.linalg.triangular_solve(lower, identity, left_side=True, lower=True)  42.9 us
    dot_general x3, matrix products, inverse_factor(): jnp.dot(matrix[half:, :half], upper_inv.T, precision=lax.Precision.HIGHEST)  36.9 us
    dot_general x1, matrix products, shards(): jnp.dot(mine, inverse.T, preferred_element_type=jnp.float32)  26.8 us
  transfers between devices with their start and end apart: 3, of which 3 were waited for; matrix products, arithmetic and copies ran while one was open for 1% of the time, Pallas kernels for 0%

profile of v1, /device:TPU:1, one launch (start us, length us, event | category | flops | bytes accessed | tf_op | source)
XLA Modules:
  0.0 1134.8 jit_solution(5611784396676347777)
XLA Ops:
  15.4 50.7 %all-gather.5.cloned.1.call-done = bf16[2048,2048]{1,0:T(8,128)(2,1)} async-done(((bf16[2048,256]{1,0:T(8,128)(2,1)}), bf16[2048,2048]{1,0:T(8,128)(2,1)}) %all-gather.5.cloned.1.call-update) | async-done | bytes 8388624 | tf_op jit(solution)/shard_map/all_gather | solution.py:62
  66.1 25.9 %while.9 = (s32[]{:T(128)}, bf16[2048,2048]{1,0:T(8,128)(2,1)}, s32[8,2]{0,1:T(2,128)S(1)}, bf16[8,128,2048]{2,1,0:T(8,128)(2,1)}, s32[]{:T(128)}) while((s32[]{:T(128)}, bf16[2048,2048]{1,0:T(8,128)(2,1)}, s32[8,2]{0,1:T(2,128)S(1)}, bf16[8,128,2048]{2,1,0:T(8,128)(2,1)}, s32[]{:T(128)}) %tuple.104), condition=%wide.while_cond.1, body=%wide.while_body.1.sunk | while | flops 2 | bytes 1049689 | solution.py:41
  101.1 197.6 %all-gather.9.cloned.1.call-done = f32[4096,2048]{1,0:T(8,128)} async-done(((f32[256,2048]{1,0:T(8,128)}), f32[4096,2048]{1,0:T(8,128)}) %all-gather.9.cloned.1.call-update) | async-done | bytes 33554448 | tf_op jit(solution)/shard_map/all_gather | solution.py:78
  298.8 11.8 %reduce_sum.9 = f32[256,2048]{1,0:T(8,128)S(1)} reduce(f32[16,256,2048]{2,1,0:T(8,128)} %bitcast.223, f32[]{:T(128)} %constant.131.clone.1), dimensions={0}, to_apply=%region_1.2 | reduce | flops 7864320 | bytes 35651588 | tf_op jit(solution)/shard_map/reduce_sum | solution.py:78
  312.8 85.0 %all-gather.7.cloned.1.call-done = f32[2048,2048]{0,1:T(8,128)} async-done(((f32[256,2048]{0,1:T(8,128)}), f32[2048,2048]{0,1:T(8,128)}) %all-gather.7.cloned.1.call-update) | async-done | bytes 16777232 | tf_op jit(solution)/shard_map/all_gather | solution.py:79
  400.9 11.7 %cholesky.462 = f32[128,128]{1,0:T(8,128)S(1)} custom-call(f32[128,128]{1,0:T(8,128)S(1)} %cholesky.746), custom_call_target="Cholesky" | custom-call | tf_op jit(solution)/shard_map/jit(cholesky)/cholesky | solution.py:14
  423.3 11.7 %cholesky.481 = f32[128,128]{1,0:T(8,128)S(1)} custom-call(f32[128,128]{1,0:T(8,128)S(1)} %cholesky.750), custom_call_target="Cholesky" | custom-call | tf_op jit(solution)/shard_map/jit(cholesky)/cholesky | solution.py:14
  445.9 11.7 %cholesky.502 = f32[128,128]{1,0:T(8,128)S(1)} custom-call(f32[128,128]{1,0:T(8,128)S(1)} %cholesky.755), custom_call_target="Cholesky" | custom-call | tf_op jit(solution)/shard_map/jit(cholesky)/cholesky | solution.py:14
  468.7 11.7 %cholesky.519 = f32[128,128]{1,0:T(8,128)S(1)} custom-call(f32[128,128]{1,0:T(8,128)S(1)} %convolution_subtract_fusion.25), custom_call_target="Cholesky" | custom-call | tf_op jit(solution)/shard_map/jit(cholesky)/cholesky | solution.py:14
  492.8 39.3 %custom-call.38 = f32[4,128,128]{1,2,0:T(8,128)S(1)} custom-call(f32[4,128,128]{2,1,0:T(8,128)S(1)} %get-tuple-element.43), custom_call_target="InvertDiagBlocksLowerTriangular" | custom-call | tf_op jit(solution)/shard_map/triangular_solve/custom-call.3 | solution.py:16
  549.8 12.1 %cholesky.534 = f32[128,128]{1,0:T(8,128)S(1)} custom-call(f32[128,128]{1,0:T(8,128)S(1)} %cholesky.759), custom_call_target="Cholesky" | custom-call | tf_op jit(solution)/shard_map/jit(cholesky)/cholesky | solution.py:14
  574.4 11.7 %cholesky.553 = f32[128,128]{1,0:T(8,128)S(1)} custom-call(f32[128,128]{1,0:T(8,128)S(1)} %cholesky.763), custom_call_target="Cholesky" | custom-call | tf_op jit(solution)/shard_map/jit(cholesky)/cholesky | solution.py:14
  598.9 11.9 %cholesky.574 = f32[128,128]{1,0:T(8,128)S(1)} custom-call(f32[128,128]{1,0:T(8,128)S(1)} %cholesky.768), custom_call_target="Cholesky" | custom-call | tf_op jit(solution)/shard_map/jit(cholesky)/cholesky | solution.py:14
  622.8 11.7 %cholesky.591 = f32[128,128]{1,0:T(8,128)S(1)} custom-call(f32[128,128]{1,0:T(8,128)S(1)} %convolution_subtract_fusion.24), custom_call_target="Cholesky" | custom-call | tf_op jit(solution)/shard_map/jit(cholesky)/cholesky | solution.py:14
  650.4 39.3 %custom-call.42 = f32[4,128,128]{1,2,0:T(8,128)S(1)} custom-call(f32[4,128,128]{2,1,0:T(8,128)S(1)} %get-tuple-element.44), custom_call_target="InvertDiagBlocksLowerTriangular" | custom-call | tf_op jit(solution)/shard_map/triangular_solve/custom-call.3 | solution.py:16
  698.4 28.6 %fusion.9 = f32[1024,1024]{1,0:T(8,128)S(1)} fusion(f32[2048,2048]{0,1:T(8,128)} %all-gather.7.cloned.1.call-done, f32[512,512]{1,0:T(8,128)S(1)} %copy-done.7, f32[128,512]{1,0:T(8,128)S(1)} %fusion.125, f32[128,512]{1,0:T(8,128)S(1)} %fusion.126, f32[128,512]{1,0:T(8,128)S(1)} %fusion.128, f32[128,512]{1,0:T(8,128)S(1)} %fusion.81, ...), kind=kOutput, calls=%fused_computation.24 | convolution fusion | flops 12892241920 | bytes 11534336 | tf_op jit(solution)/shard_map/dot_general | solution.py:19
  727.0 16.8 %fusion.172 = f32[1024,1024]{1,0:T(8,128)} fusion(f32[1024,1024]{1,0:T(8,128)S(1)} %fusion.9, f32[512,512]{1,0:T(8,128)S(1)} %copy-done.7, f32[128,512]{1,0:T(8,128)S(1)} %fusion.125, f32[128,512]{1,0:T(8,128)S(1)} %fusion.126, f32[128,512]{1,0:T(8,128)S(1)} %fusion.128, f32[128,512]{1,0:T(8,128)S(1)} %fusion.81, f32[512,512]{1,0:T(8,128)S(1)} %convolution_negate_fusion.1), kind=kOutput, calls=%fused_computation.324 | convolution fusion | flops 12892241920 | bytes 11534336 | tf_op jit(solution)/shard_map/dot_general | solution.py:24
  743.8 16.0 %slice_subtract_fusion = f32[1024,1024]{0,1:T(8,128)S(1)} fusion(f32[2048,2048]{0,1:T(8,128)} %all-gather.7.cloned.1.call-done, f32[1024,1024]{1,0:T(8,128)S(1)} %fusion.9), kind=kOutput, calls=%fused_computation.26 | convolution fusion | flops 12885950464 | bytes 16777216 | tf_op jit(solution)/shard_map/dot_general | solution.py:20
  766.9 11.7 %cholesky.606 = f32[128,128]{1,0:T(8,128)S(1)} custom-call(f32[128,128]{1,0:T(8,128)S(1)} %cholesky.772), custom_call_target="Cholesky" | custom-call | tf_op jit(solution)/shard_map/jit(cholesky)/cholesky | solution.py:14
  791.1 11.7 %cholesky.625 = f32[128,128]{1,0:T(8,128)S(1)} custom-call(f32[128,128]{1,0:T(8,128)S(1)} %cholesky.776), custom_call_target="Cholesky" | custom-call | tf_op jit(solution)/shard_map/jit(cholesky)/cholesky | solution.py:14
  815.8 11.7 %cholesky.646 = f32[128,128]{1,0:T(8,128)S(1)} custom-call(f32[128,128]{1,0:T(8,128)S(1)} %cholesky.781), custom_call_target="Cholesky" | custom-call | tf_op jit(solution)/shard_map/jit(cholesky)/cholesky | solution.py:14
  839.4 11.7 %cholesky.663 = f32[128,128]{1,0:T(8,128)S(1)} custom-call(f32[128,128]{1,0:T(8,128)S(1)} %convolution_subtract_fusion.23), custom_call_target="Cholesky" | custom-call | tf_op jit(solution)/shard_map/jit(cholesky)/cholesky | solution.py:14
  856.0 11.8 %while.12 = (s32[]{:T(128)}, f32[512,512]{1,0:T(8,128)}, s32[4,2]{0,1:T(2,128)S(1)}, f32[4,128,128]{2,1,0:T(8,128)S(1)}, s32[]{:T(128)}) while((s32[]{:T(128)}, f32[512,512]{1,0:T(8,128)}, s32[4,2]{0,1:T(2,128)S(1)}, f32[4,128,128]{2,1,0:T(8,128)S(1)}, s32[]{:T(128)}) %tuple.126), condition=%wide.while_cond.clone.1, body=%wide.while_body.clone.1.sunk | while | flops 2 | bytes 131181 | solution.py:16
  867.9 39.3 %custom-call.46 = f32[4,128,128]{1,2,0:T(8,128)S(1)} custom-call(f32[4,128,128]{2,1,0:T(8,128)S(1)} %get-tuple-element.45), custom_call_target="InvertDiagBlocksLowerTriangular" | custom-call | tf_op jit(solution)/shard_map/triangular_solve/custom-call.3 | solution.py:16
  933.6 11.7 %cholesky.678 = f32[128,128]{1,0:T(8,128)S(1)} custom-call(f32[128,128]{1,0:T(8,128)S(1)} %cholesky.785), custom_call_target="Cholesky" | custom-call | tf_op jit(solution)/shard_map/jit(cholesky)/cholesky | solution.py:14
  957.8 11.7 %cholesky.697 = f32[128,128]{1,0:T(8,128)S(1)} custom-call(f32[128,128]{1,0:T(8,128)S(1)} %cholesky.789), custom_call_target="Cholesky" | custom-call | tf_op jit(solution)/shard_map/jit(cholesky)/cholesky | solution.py:14
  982.6 11.7 %cholesky.718 = f32[128,128]{1,0:T(8,128)S(1)} custom-call(f32[128,128]{1,0:T(8,128)S(1)} %cholesky.794), custom_call_target="Cholesky" | custom-call | tf_op jit(solution)/shard_map/jit(cholesky)/cholesky | solution.py:14
  1006.4 11.7 %cholesky.735 = f32[128,128]{1,0:T(8,128)S(1)} custom-call(f32[128,128]{1,0:T(8,128)S(1)} %convolution_subtract_fusion.22), custom_call_target="Cholesky" | custom-call | tf_op jit(solution)/shard_map/jit(cholesky)/cholesky | solution.py:14
  1022.6 11.8 %while.13 = (s32[]{:T(128)}, f32[512,512]{1,0:T(8,128)}, s32[4,2]{0,1:T(2,128)S(1)}, f32[4,128,128]{2,1,0:T(8,128)S(1)}, s32[]{:T(128)}) while((s32[]{:T(128)}, f32[512,512]{1,0:T(8,128)}, s32[4,2]{0,1:T(2,128)S(1)}, f32[4,128,128]{2,1,0:T(8,128)S(1)}, s32[]{:T(128)}) %tuple.127), condition=%wide.while_cond.clone.2, body=%wide.while_body.clone.2.sunk | while | flops 2 | bytes 131181 | solution.py:16
  1034.4 39.3 %custom-call.50 = f32[4,128,128]{1,2,0:T(8,128)S(1)} custom-call(f32[4,128,128]{2,1,0:T(8,128)S(1)} %get-tuple-element.46), custom_call_target="InvertDiagBlocksLowerTriangular" | custom-call | tf_op jit(solution)/shard_map/triangular_solve/custom-call.3 | solution.py:16
  1087.5 13.6 %negate_convert_fusion = bf16[1024,1024]{1,0:T(8,128)(2,1)S(1)} fusion(f32[1024,1024]{1,0:T(8,128)S(1)} %copy-done.19, f32[512,512]{1,0:T(8,128)S(1)} %copy-done.9, f32[128,512]{1,0:T(8,128)S(1)} %fusion.113, f32[128,512]{1,0:T(8,128)S(1)} %fusion.114, f32[128,512]{1,0:T(8,128)S(1)} %fusion.116, f32[128,512]{1,0:T(8,128)S(1)} %fusion.77, ...), kind=kOutput, calls=%fused_computation.30 | convolution fusion | flops 12894339072 | bytes 9437184 | tf_op jit(solution)/shard_map/dot_general | solution.py:22
  1101.1 26.8 %fusion.13 = bf16[256,2048]{1,0:T(8,128)(2,1)} fusion(bf16[1024,1024]{1,0:T(8,128)(2,1)S(1)} %copy-done.17, bf16[1024,1024]{1,0:T(8,128)(2,1)S(1)} %fusion.16, bf16[1024,1024]{1,0:T(8,128)(2,1)S(1)} %negate_convert_fusion, bf16[2048,2048]{1,0:T(8,128)(2,1)} %get-tuple-element.366, s32[]{:T(128)S(6)} %select_n.31), kind=kOutput, calls=%fused_computation.34 | convolution fusion | flops 2181562368 | bytes 8388612 | tf_op jit(solution)/shard_map/dot_general | solution.py:83
  (283 shorter events, 336.6 us)
Async XLA Ops:
  6.5 5.3 copy-start
  6.5 59.5 %all-gather.5.cloned.1.call-start = ((), (), s32[]{:S(2)}) async-start(), calls=%async_computation | async-start | bytes 9437184 | tf_op jit(solution)/shard_map/all_gather | solution.py:62
  7.3 291.5 %all-gather.9.cloned.1.call-start = ((), (), s32[]{:S(2)}) async-start(), calls=%async_computation.2 | async-start | bytes 35651584 | tf_op jit(solution)/shard_map/all_gather | solution.py:78
  91.9 5.4 copy-start.2
  94.9 2.4 copy-start.3
  101.1 296.7 %all-gather.7.cloned.1.call-start = ((), (), s32[]{:S(2)}) async-start(), calls=%async_computation.1 | async-start | bytes 18874368 | tf_op jit(solution)/shard_map/all_gather | solution.py:79
  548.9 1.0 copy-start.12
  689.7 3.5 copy-start.18
  690.2 8.2 copy-start.7
  696.5 30.5 %copy-start.15 = (f32[128,512]{1,0:T(8,128)}, f32[128,512]{1,0:T(8,128)S(1)}, u32[]{:S(2)}) copy-start(f32[128,512]{1,0:T(8,128)S(1)} %fusion.125) | copy-start | bytes 786436
  698.4 28.7 %copy-start.4 = (f32[512,512]{1,0:T(8,128)}, f32[512,512]{1,0:T(8,128)S(1)}, u32[]{:S(2)}) copy-start(f32[512,512]{1,0:T(8,128)S(1)} %convolution_negate_fusion.1) | copy-start | bytes 3145732
  759.9 2.0 copy-start.10
  765.9 1.0 copy-start.14
  907.2 7.1 copy-start.11
  917.8 4.8 copy-start.5
  917.9 4.8 copy-start.8
  917.9 4.8 copy-start.16
  932.6 1.0 copy-start.13
  1021.3 58.3 %copy-start.6 = (f32[512,512]{1,0:T(8,128)S(1)}, f32[512,512]{1,0:T(8,128)}, u32[]{:S(2)}) copy-start(f32[512,512]{1,0:T(8,128)} %fusion.170) | copy-start | bytes 3145732
  1074.1 7.4 copy-start.9
  1079.7 7.9 copy-start.19
  1087.5 13.6 %copy-start.17 = (bf16[1024,1024]{1,0:T(8,128)(2,1)S(1)}, bf16[1024,1024]{1,0:T(8,128)(2,1)}, u32[]{:S(2)}) copy-start(bf16[1024,1024]{1,0:T(8,128)(2,1)} %fusion.173) | copy-start | bytes 6291460
  1101.1 26.8 %copy-start.1 = (bf16[128,8,128]{2,1,0:T(8,128)(2,1)S(1)}, bf16[128,8,128]{2,1,0:T(8,128)(2,1)}, u32[]{:S(2)}) copy-start(bf16[128,8,128]{2,1,0:T(8,128)(2,1)} %param.10) | copy-start | bytes 786436
Sparse Core Ops, SparseCore 0:
  9.0 57.0 all-gather.4
  101.2 197.4 all-gather.8
  312.8 84.9 all-gather.6
